TPU v7x, 32 devices: a whole 2x2x4 slice. The times are simulated.
32 devices in a mesh: rep: 4 (over z), tp: 8 (over y, x, core).
Axes of the slice: x: 2, y: 2, z: 4, core: 2. Of those that a mesh axis runs over, the one named last changes fastest.
Arguments:
- exp_hidden: bfloat16 [256, 8192], P('rep', 'tp'), may hold values from -160 to 160
- exp_pre_gain: float32 [8192], P('tp'), may hold values from 0.25 to 1.75
- exp_gate: bfloat16 [8192, 28672], P('tp', 'rep'), may hold values from -0.0625 to 0.0625
- exp_up: bfloat16 [8192, 28672], P('tp', 'rep'), may hold values from -0.0625 to 0.0625
- exp_down: bfloat16 [28672, 8192], P('rep', 'tp'), may hold values from -0.03125 to 0.03125
- exp_out_gain: float32 [8192], P('tp'), may hold values from 0.25 to 1.75
- exp_head: bfloat16 [8192, 65536], P(None, ('rep', 'tp')), may hold values from -10 to 10
- ama_hidden: bfloat16 [256, 4096], P('rep', 'tp'), may hold values from -160 to 160
- ama_out_gain: float32 [4096], P('tp'), may hold values from 0.25 to 1.75
- ama_head: bfloat16 [4096, 65536], P(None, ('rep', 'tp')), may hold values from -10 to 10
- logit_scale: float32 [256], replicated, may hold values from 0.25 to 3
- prompt_of: int32 [256], replicated, may hold values from 0 to 7
- prior_picks: int32 [8, 24], replicated, may hold values from 0 to 65535
- valid_mask: int32 [65536], P(('rep', 'tp')), may hold values 0 or 1
Outputs:
- scores: float32 [256, 65536], P(None, ('rep', 'tp'))
- beam_best: float32 [256], replicated
All inputs are finite; a program needn't handle non-finite values. No bound on the sum of `valid_mask` on one device may be relied on, other than what follows from the above.
Results may differ from a plain program's by a relative error of at most 0.0034.
Values may be sent and summed in bfloat16 or wider, within the bound.
No kernel may reach another device: no remote copies, remote signals or barrier semaphores. Data moves between devices by JAX's collectives and lax.ppermute only.
A program may use at most 192 MiB of HBM per device.

v0:
```python
import jax
import jax.numpy as jnp
from jax import lax
from jax.sharding import PartitionSpec as P

DE = 8192
DA = 4096
norm_epsilon = 1e-05
contrast_weight = 0.5
hamming_weight = 0.7


def scaled_rows(values, squares, width, gain):
    return (values * lax.rsqrt(squares[:, None] / width + norm_epsilon) * gain).astype(jnp.bfloat16)


def both_halves(rows_in, gate_weight, up_weight):
    gate = jnp.dot(rows_in, gate_weight, preferred_element_type=jnp.float32)
    up = jnp.dot(rows_in, up_weight, preferred_element_type=jnp.float32)
    return jnp.concatenate([gate, up], axis=1)


def gated_rows(summed, width):
    return (jax.nn.silu(summed[:, :width]) * summed[:, width:]).astype(jnp.bfloat16)


def body(
    exp_hidden,
    exp_pre_gain,
    exp_gate,
    exp_up,
    exp_down,
    exp_out_gain,
    exp_head,
    ama_hidden,
    ama_out_gain,
    ama_head,
    logit_scale,
    prompt_of,
    prior_picks,
    valid_mask,
):
    values_exp = exp_hidden.astype(jnp.float32)
    values_ama = ama_hidden.astype(jnp.float32)
    squares_exp = lax.psum(jnp.sum(values_exp * values_exp, axis=1), "tp")
    normed_exp = scaled_rows(values_exp, squares_exp, DE, exp_pre_gain)
    rows_exp = lax.all_gather(normed_exp, "rep", axis=0, tiled=True)
    width_exp = exp_gate.shape[1]
    summed_exp = lax.psum_scatter(
        both_halves(rows_exp, exp_gate, exp_up), "tp", scatter_dimension=0, tiled=True
    )
    hidden_exp = gated_rows(summed_exp, width_exp)
    term_exp = jnp.dot(
        lax.all_gather(hidden_exp, "tp", axis=0, tiled=True),
        exp_down,
        preferred_element_type=jnp.float32,
    )
    out_exp = lax.psum_scatter(term_exp, "rep", scatter_dimension=0, tiled=True)
    layer_exp = values_exp + out_exp
    final_sq_exp, final_sq_ama = lax.psum(
        (jnp.sum(layer_exp * layer_exp, axis=1), jnp.sum(values_ama * values_ama, axis=1)), "tp"
    )
    final_exp = scaled_rows(layer_exp, final_sq_exp, DE, exp_out_gain)
    final_ama = scaled_rows(values_ama, final_sq_ama, DA, ama_out_gain)
    features_exp, features_ama = (
        lax.all_gather(final_exp, "tp", axis=1, tiled=True),
        lax.all_gather(final_ama, "tp", axis=1, tiled=True),
    )
    full_exp, full_ama = (
        lax.all_gather(features_exp, "rep", axis=0, tiled=True),
        lax.all_gather(features_ama, "rep", axis=0, tiled=True),
    )
    logits_exp = logit_scale[:, None] * jnp.dot(
        full_exp, exp_head, preferred_element_type=jnp.float32
    )
    logits_ama = logit_scale[:, None] * jnp.dot(
        full_ama, ama_head, preferred_element_type=jnp.float32
    )
    top_exp, top_ama = lax.pmax(
        (jnp.max(logits_exp, axis=1), jnp.max(logits_ama, axis=1)), ("rep", "tp")
    )
    local_exp = jnp.sum(jnp.exp(logits_exp - top_exp[:, None]), axis=1)
    local_ama = jnp.sum(jnp.exp(logits_ama - top_ama[:, None]), axis=1)
    total_exp, total_ama = lax.psum((local_exp, local_ama), ("rep", "tp"))
    logp_exp = logits_exp - top_exp[:, None] - jnp.log(total_exp)[:, None]
    logp_ama = logits_ama - top_ama[:, None] - jnp.log(total_ama)[:, None]
    entries = exp_head.shape[1]
    first_entry = lax.axis_index(("rep", "tp")) * entries
    vocab_ids = first_entry + jnp.arange(entries, dtype=jnp.int32)
    picks_row = jnp.take(prior_picks, prompt_of, axis=0)
    counts = jnp.sum(
        (picks_row[:, :, None] == vocab_ids[None, None, :]).astype(jnp.float32), axis=1
    )
    valid = valid_mask.astype(jnp.float32)[None, :]
    scores = logp_exp - contrast_weight * valid * logp_ama - hamming_weight * counts
    beam_best = lax.pmax(jnp.max(scores, axis=1), ("rep", "tp"))
    return (scores, beam_best)


def solution(mesh):
    placed = (
        P("rep", "tp"),
        P("tp"),
        P("tp", "rep"),
        P("tp", "rep"),
        P("rep", "tp"),
        P("tp"),
        P(None, ("rep", "tp")),
        P("rep", "tp"),
        P("tp"),
        P(None, ("rep", "tp")),
        P(),
        P(),
        P(),
        P(("rep", "tp")),
    )
    return jax.shard_map(
        body, mesh=mesh, in_specs=placed, out_specs=(P(None, ("rep", "tp")), P()), check_vma=False
    )
```

profile of v0, /device:TPU:0, one launch (start us, length us, event | category | flops | bytes accessed | tf_op | source)
XLA Modules:
  0.0 552.7 jit_solution(7237676692740054795)
XLA Ops:
  7.2 0.0 copy-start
  7.2 0.0 reduce-scatter.3.cloned.1.call-start
  7.2 1.0 fusion.1
  8.3 15.2 %psum.35 = f32[64]{0:T(128)S(1)} all-reduce(f32[64]{0:T(128)S(1)} %fusion.1), channel_id=1, replica_groups=mesh['rep'=4,'tp'=8] {'tp'}, use_global_device_ids=true, to_apply=%region_1.0 | all-reduce | flops 64 | bytes 512 | tf_op jit(solution)/shard_map/psum | solution.py:45
  23.4 1.0 fusion.3
  24.4 15.9 %all_gather.18 = bf16[256,1024]{1,0:T(8,128)(2,1)S(1)} all-gather(bf16[64,1024]{1,0:T(8,128)(2,1)S(1)} %fusion.3), channel_id=1, replica_groups=mesh['rep'=4,'tp'=8] {'rep'}, dimensions={0}, use_global_device_ids=true | all-gather | bytes 655360 | tf_op jit(solution)/shard_map/all_gather | solution.py:47
  40.4 7.4 %fusion.10 = f32[256,7168]{1,0:T(8,128)S(1)} fusion(bf16[256,1024]{1,0:T(8,128)(2,1)S(1)} %all_gather.18, bf16[1024,7168]{1,0:T(8,128)(2,1)} %param.16), kind=kOutput, calls=%fused_computation.35 | convolution fusion | flops 3758096384 | bytes 22544384 | tf_op jit(solution)/shard_map/dot_general | solution.py:18
  47.8 1.9 copy-done.2
  49.7 4.1 fusion.11
  53.8 5.5 pad_maximum_fusion
  59.3 0.0 reduce-scatter.3.cloned.1.call-update
  59.3 0.0 all-gather.5.cloned.1.call-start
  59.3 103.7 %reduce-scatter.3.cloned.1.call-done = f32[32,14336]{1,0:T(8,128)} async-done(((f32[256,14336]{1,0:T(8,128)}), f32[32,14336]{1,0:T(8,128)}) %reduce-scatter.3.cloned.1.call-update) | async-done | bytes 1835024 | tf_op jit(solution)/shard_map/reduce_scatter | solution.py:49
  163.1 2.5 fusion
  165.6 0.0 all-gather.5.cloned.1.call-update
  165.6 0.0 copy-start.6
  165.6 0.0 copy-start.7
  165.6 0.0 reduce-scatter.5.cloned.1.call-start
  165.7 34.4 %all-gather.5.cloned.1.call-done = bf16[256,7168]{1,0:T(8,128)(2,1)} async-done(((bf16[32,7168]{1,0:T(8,128)(2,1)}), bf16[256,7168]{1,0:T(8,128)(2,1)}) %all-gather.5.cloned.1.call-update) | async-done | bytes 3670032 | tf_op jit(solution)/shard_map/all_gather | solution.py:54
  200.1 11.2 %fusion.12 = f32[256,1024]{1,0:T(8,128)} fusion(bf16[256,7168]{1,0:T(8,128)(2,1)} %all-gather.5.cloned.1.call-done, bf16[7168,1024]{1,0:T(8,128)(2,1)} %param.18), kind=kOutput, calls=%fused_computation.37 | convolution fusion | flops 3758096384 | bytes 19398656 | tf_op jit(solution)/shard_map/dot_general | solution.py:53
  211.3 0.0 reduce-scatter.5.cloned.1.call-update
  211.4 0.0 copy-start.9
  211.4 0.0 all-gather.7.cloned.1.call-start
  211.4 0.1 fusion.4
  211.5 27.3 %reduce-scatter.5.cloned.1.call-done = f32[64,1024]{1,0:T(8,128)} async-done(((f32[256,1024]{1,0:T(8,128)}), f32[64,1024]{1,0:T(8,128)}) %reduce-scatter.5.cloned.1.call-update) | async-done | bytes 262160 | tf_op jit(solution)/shard_map/reduce_scatter | solution.py:58
  238.8 1.1 multiply_reduce_fusion
  239.9 13.2 %all-reduce.2 = (f32[64]{0:T(128)S(1)}, f32[64]{0:T(128)S(1)}) all-reduce(f32[64]{0:T(128)S(1)} %fusion.4, f32[64]{0:T(128)S(1)} %multiply_reduce_fusion), channel_id=1, replica_groups=mesh['rep'=4,'tp'=8] {'tp'}, use_global_device_ids=true, to_apply=%region_11.12 | all-reduce | flops 128 | bytes 1024 | tf_op jit(solution)/shard_map/psum | solution.py:60
  253.1 1.7 multiply_convert_fusion
  254.8 0.0 all-gather.7.cloned.1.call-update
  254.8 0.0 all-gather.11.cloned.1.call-start
  254.9 0.1 fusion.6
  255.0 10.5 %all_gather.22 = bf16[64,4096]{1,0:T(8,128)(2,1)} all-gather(bf16[64,512]{1,0:T(8,128)(2,1)S(1)} %fusion.6), channel_id=1, replica_groups=mesh['rep'=4,'tp'=8] {'tp'}, dimensions={1}, use_global_device_ids=true | all-gather | bytes 589824 | tf_op jit(solution)/shard_map/all_gather | solution.py:67
  265.5 0.0 all-gather.11.cloned.1.call-update
  265.6 0.2 all-gather.9.cloned.1.call-start
  265.8 9.6 %all-gather.7.cloned.1.call-done = bf16[64,8192]{1,0:T(8,128)(2,1)} async-done(((bf16[64,1024]{1,0:T(8,128)(2,1)}), bf16[64,8192]{1,0:T(8,128)(2,1)}) %all-gather.7.cloned.1.call-update) | async-done | bytes 1048592 | tf_op jit(solution)/shard_map/all_gather | solution.py:66
  275.4 0.0 all-gather.9.cloned.1.call-update
  275.5 0.7 gather_fusion
  276.3 0.1 broadcast_select_fusion
  276.4 20.6 %convert_reduce_fusion = f32[256,2048]{1,0:T(8,128)} fusion(s32[2048]{0:T(1024)S(1)} %iota_add_fusion, s32[256,24]{1,0:T(8,128)S(1)} %broadcast_select_fusion), kind=kLoop, calls=%fused_computation.1 | loop fusion | flops 37224448 | bytes 2129920 | tf_op jit(solution)/shard_map/reduce_sum | solution.py:91
  297.0 25.5 %all-gather.11.cloned.1.call-done = bf16[256,4096]{1,0:T(8,128)(2,1)} async-done(((bf16[64,4096]{1,0:T(8,128)(2,1)}), bf16[256,4096]{1,0:T(8,128)(2,1)}) %all-gather.11.cloned.1.call-update) | async-done | bytes 2097168 | tf_op jit(solution)/shard_map/all_gather | solution.py:71
  322.5 8.8 %fusion.8 = (f32[256]{0:T(256)S(1)}, f32[256,2048]{1,0:T(8,128)S(1)}) fusion(bf16[256,4096]{1,0:T(8,128)(2,1)} %all-gather.11.cloned.1.call-done, bf16[4096,2048]{1,0:T(8,128)(2,1)} %param.23, f32[256]{0:T(256)S(1)} %copy-done.9), kind=kOutput, calls=%fused_computation.33 | convolution fusion | flops 4296015872 | bytes 20973568 | tf_op jit(solution)/shard_map/dot_general | solution.py:76
  331.3 72.2 %all-gather.9.cloned.1.call-done = bf16[256,8192]{1,0:T(8,128)(2,1)} async-done(((bf16[64,8192]{1,0:T(8,128)(2,1)}), bf16[256,8192]{1,0:T(8,128)(2,1)}) %all-gather.9.cloned.1.call-update) | async-done | bytes 4194320 | tf_op jit(solution)/shard_map/all_gather | solution.py:70
  403.5 17.2 %fusion.9 = (f32[256]{0:T(256)S(1)}, f32[256,2048]{1,0:T(8,128)}) fusion(bf16[256,8192]{1,0:T(8,128)(2,1)} %all-gather.9.cloned.1.call-done, bf16[8192,2048]{1,0:T(8,128)(2,1)} %param.20, f32[256]{0:T(256)S(1)} %copy-done.9), kind=kOutput, calls=%fused_computation.34 | convolution fusion | flops 8590983168 | bytes 39847936 | tf_op jit(solution)/shard_map/dot_general | solution.py:73
  420.7 38.6 %all-reduce.1 = (f32[256]{0:T(256)S(1)}, f32[256]{0:T(256)S(1)}) all-reduce(f32[256]{0:T(256)S(1)} %get-tuple-element.10, f32[256]{0:T(256)S(1)} %get-tuple-element.12), channel_id=1, replica_groups=mesh['rep'=4,'tp'=8] {'rep','tp'}, use_global_device_ids=true, to_apply=%region_13.14 | all-reduce | flops 512 | bytes 4096 | tf_op jit(solution)/shard_map/pmax | solution.py:79
  459.4 2.3 exponential_reduce_fusion
  461.7 40.4 %all-reduce = (f32[256]{0:T(256)S(1)}, f32[256]{0:T(256)S(1)}) all-reduce(f32[256]{0:T(256)S(1)} %get-tuple-element.14, f32[256]{0:T(256)S(1)} %get-tuple-element.15), channel_id=1, replica_groups=mesh['rep'=4,'tp'=8] {'rep','tp'}, use_global_device_ids=true, to_apply=%region_15.16 | all-reduce | flops 512 | bytes 4096 | tf_op jit(solution)/shard_map/psum | solution.py:84
  502.1 4.4 fusion.7
  506.5 39.4 %pmax.23 = f32[256]{0:T(256)} all-reduce(f32[256]{0:T(256)S(1)} %get-tuple-element.8), channel_id=1, replica_groups=mesh['rep'=4,'tp'=8] {'rep','tp'}, use_global_device_ids=true, to_apply=%region_18.19 | all-reduce | flops 256 | bytes 2048 | tf_op jit(solution)/shard_map/pmax | solution.py:96
  (25 shorter events, 0.1 us)
Async XLA Ops:
  7.2 268.3 %copy-start = (s32[8,24]{1,0:T(8,128)S(1)}, s32[8,24]{1,0:T(8,128)}, u32[]{:S(2)}) copy-start(s32[8,24]{1,0:T(8,128)} %param.26) | copy-start | bytes 2308
  7.2 155.9 %reduce-scatter.3.cloned.1.call-start = ((), (), s32[]{:S(2)}) async-start(), calls=%async_computation.2 | async-start | bytes 16515072 | tf_op jit(solution)/shard_map/reduce_scatter | solution.py:49
  40.4 9.3 %copy-start.2 = (bf16[1024,7168]{1,0:T(8,128)(2,1)S(1)}, bf16[1024,7168]{1,0:T(8,128)(2,1)}, u32[]{:S(2)}) copy-start(bf16[1024,7168]{1,0:T(8,128)(2,1)} %param.17) | copy-start | bytes 44040196
  59.3 140.8 %all-gather.5.cloned.1.call-start = ((), (), s32[]{:S(2)}) async-start(), calls=%async_computation.3 | async-start | bytes 4128768 | tf_op jit(solution)/shard_map/all_gather | solution.py:54
  165.6 45.8 %copy-start.4 = (bf16[64,512]{1,0:T(8,128)(2,1)S(1)}, bf16[64,512]{1,0:T(8,128)(2,1)}, u32[]{:S(2)}) copy-start(bf16[64,512]{1,0:T(8,128)(2,1)} %param.21) | copy-start | bytes 196612
  165.6 73.2 %copy-start.3 = (bf16[64,1024]{1,0:T(8,128)(2,1)S(1)}, bf16[64,1024]{1,0:T(8,128)(2,1)}, u32[]{:S(2)}) copy-start(bf16[64,1024]{1,0:T(8,128)(2,1)} %param.14) | copy-start | bytes 393220
  165.6 87.5 %copy-start.6 = (f32[1024]{0:T(1024)S(1)}, f32[1024]{0:T(1024)}, u32[]{:S(2)}) copy-start(f32[1024]{0:T(1024)} %param.19) | copy-start | bytes 12292
  165.6 89.3 %copy-start.7 = (f32[512]{0:T(512)S(1)}, f32[512]{0:T(512)}, u32[]{:S(2)}) copy-start(f32[512]{0:T(512)} %param.22) | copy-start | bytes 6148
  165.6 73.2 %reduce-scatter.5.cloned.1.call-start = ((), (), s32[]{:S(2)}) async-start(), calls=%async_computation.4 | async-start | bytes 1310720 | tf_op jit(solution)/shard_map/reduce_scatter | solution.py:58
  211.3 64.1 %copy-start.8 = (s32[256]{0:T(256)S(1)}, s32[256]{0:T(256)}, u32[]{:S(2)}) copy-start(s32[256]{0:T(256)} %param.25) | copy-start | bytes 3076
  211.3 64.9 %copy-start.5 = (s32[2048]{0:T(1024)S(1)}, s32[2048]{0:T(1024)}, u32[]{:S(2)}) copy-start(s32[2048]{0:T(1024)} %param.27) | copy-start | bytes 24580
  211.4 111.2 %copy-start.9 = (f32[256]{0:T(256)S(1)}, f32[256]{0:T(256)}, u32[]{:S(2)}) copy-start(f32[256]{0:T(256)} %param.24) | copy-start | bytes 3076
  211.4 64.0 %all-gather.7.cloned.1.call-start = ((), (), s32[]{:S(2)}) async-start(), calls=%async_computation.5 | async-start | bytes 1179648 | tf_op jit(solution)/shard_map/all_gather | solution.py:66
  254.8 67.7 %all-gather.11.cloned.1.call-start = ((), (), s32[]{:S(2)}) async-start(), calls=%async_computation.7 | async-start | bytes 2621440 | tf_op jit(solution)/shard_map/all_gather | solution.py:71
  265.6 138.0 %all-gather.9.cloned.1.call-start = ((), (), s32[]{:S(2)}) async-start(), calls=%async_computation.6 | async-start | bytes 5242880 | tf_op jit(solution)/shard_map/all_gather | solution.py:70
  502.1 43.8 %copy-start.1 = (s32[8,24]{1,0:T(8,128)S(1)}, s32[8,24]{1,0:T(8,128)}, u32[]{:S(2)}) copy-start(s32[8,24]{1,0:T(8,128)} %param.26) | copy-start | bytes 2308
Sparse Core Ops, SparseCore 0:
  59.4 103.6 reduce-scatter.2
  165.7 34.3 all-gather.4
  211.5 27.2 reduce-scatter.4
  255.0 20.3 all-gather.6
  276.8 45.6 all-gather.10
  323.9 79.5 all-gather.8
where the time goes:
time: 553 us
  waiting for transfers between devices  273 us (49%)
  blocking collectives  173 us (31%)
  matrix products  48.7 us (9%)
  other arithmetic  40.4 us (7%)
  between operations  14.3 us (3%)
    reduce_scatter x1, waiting for transfers between devices, body(): lax.psum_scatter(both_halves(rows_exp, exp_gate, exp_up), 'tp', scatter_d...  104 us
    all_gather x1, waiting for transfers between devices, body(): lax.all_gather(features_exp, 'rep', axis=0, tiled=True)  72.2 us
    psum x1, blocking collectives, body(): total_exp, total_ama = lax.psum((local_exp, local_ama), ('rep', 'tp'))  40.4 us
    pmax x1, blocking collectives, body(): beam_best = lax.pmax(jnp.max(scores, axis=1), ('rep', 'tp'))  39.4 us
    pmax x1, blocking collectives, body(): lax.pmax((jnp.max(logits_exp, axis=1), jnp.max(logits_ama, axis=1)), ('re...  38.6 us
    all_gather x1, waiting for transfers between devices, body(): lax.all_gather(hidden_exp, 'tp', axis=0, tiled=True)  34.4 us
    reduce_scatter x1, waiting for transfers between devices, body(): out_exp = lax.psum_scatter(term_exp, 'rep', scatter_dimension=0, tiled=True)  27.3 us
    all_gather x1, waiting for transfers between devices, body(): lax.all_gather(features_ama, 'rep', axis=0, tiled=True)  25.5 us
  transfers between devices with their start and end apart: 6, of which 6 were waited for; matrix products, arithmetic and copies ran while one was open for 6% of the time, Pallas kernels for 0%

commit v1 on v0

--- a/solution.py
+++ b/solution.py
@@ -81,7 +81,7 @@
     )
     local_exp = jnp.sum(jnp.exp(logits_exp - top_exp[:, None]), axis=1)
     local_ama = jnp.sum(jnp.exp(logits_ama - top_ama[:, None]), axis=1)
-    total_exp, total_ama = lax.psum((local_exp, local_ama), ("rep", "tp"))
+    total_exp, total_ama = lax.psum(lax.psum((local_exp, local_ama), "tp"), "rep")
     logp_exp = logits_exp - top_exp[:, None] - jnp.log(total_exp)[:, None]
     logp_ama = logits_ama - top_ama[:, None] - jnp.log(total_ama)[:, None]
     entries = exp_head.shape[1]

time: 553 us -> 534 us (0.966)
  blocking collectives: 173 us -> 154 us
    psum x1 -> x2, blocking collectives: 40.4 us -> 23.3 us  [the longest x1 12.7 us: body(): lax.psum((local_exp, local_ama), 'tp')]
where the time goes in v1:
time: 534 us
  waiting for transfers between devices  273 us (51%)
  blocking collectives  154 us (29%)
  matrix products  48.7 us (9%)
  other arithmetic  40.4 us (8%)
  between operations  14.3 us (3%)
    reduce_scatter x1, waiting for transfers between devices, body(): lax.psum_scatter(both_halves(rows_exp, exp_gate, exp_up), 'tp', scatter_d...  104 us
    all_gather x1, waiting for transfers between devices, body(): lax.all_gather(features_exp, 'rep', axis=0, tiled=True)  72.2 us
    pmax x1, blocking collectives, body(): lax.pmax((jnp.max(logits_exp, axis=1), jnp.max(logits_ama, axis=1)), ('re...  38.6 us
    pmax x1, blocking collectives, body(): beam_best = lax.pmax(jnp.max(scores, axis=1), ('rep', 'tp'))  37.4 us
    all_gather x1, waiting for transfers between devices, body(): lax.all_gather(hidden_exp, 'tp', axis=0, tiled=True)  34.4 us
    reduce_scatter x1, waiting for transfers between devices, body(): out_exp = lax.psum_scatter(term_exp, 'rep', scatter_dimension=0, tiled=True)  27.3 us
    all_gather x1, waiting for transfers between devices, body(): lax.all_gather(features_ama, 'rep', axis=0, tiled=True)  25.5 us
    reduce_sum x1, other arithmetic, body(): jnp.sum((picks_row[:, :, None] == vocab_ids[None, None, :]).astype(jnp.fl...  20.6 us
  transfers between devices with their start and end apart: 6, of which 6 were waited for; matrix products, arithmetic and copies ran while one was open for 6% of the time, Pallas kernels for 0%

profile of v1, /device:TPU:0, one launch (start us, length us, event | category | flops | bytes accessed | tf_op | source)
XLA Modules:
  0.0 533.6 jit_solution(4284419551679226307)
XLA Ops:
  7.2 0.0 copy-start
  7.2 0.0 reduce-scatter.3.cloned.1.call-start
  7.2 1.0 fusion.1
  8.3 15.2 %psum.49 = f32[64]{0:T(128)S(1)} all-reduce(f32[64]{0:T(128)S(1)} %fusion.1), channel_id=1, replica_groups=mesh['rep'=4,'tp'=8] {'tp'}, use_global_device_ids=true, to_apply=%region_1.0 | all-reduce | flops 64 | bytes 512 | tf_op jit(solution)/shard_map/psum | solution.py:45
  23.4 1.0 fusion.3
  24.4 15.9 %all_gather.18 = bf16[256,1024]{1,0:T(8,128)(2,1)S(1)} all-gather(bf16[64,1024]{1,0:T(8,128)(2,1)S(1)} %fusion.3), channel_id=1, replica_groups=mesh['rep'=4,'tp'=8] {'rep'}, dimensions={0}, use_global_device_ids=true | all-gather | bytes 655360 | tf_op jit(solution)/shard_map/all_gather | solution.py:47
  40.4 7.4 %fusion.10 = f32[256,7168]{1,0:T(8,128)S(1)} fusion(bf16[256,1024]{1,0:T(8,128)(2,1)S(1)} %all_gather.18, bf16[1024,7168]{1,0:T(8,128)(2,1)} %param.16), kind=kOutput, calls=%fused_computation.35 | convolution fusion | flops 3758096384 | bytes 22544384 | tf_op jit(solution)/shard_map/dot_general | solution.py:18
  47.8 1.9 copy-done.2
  49.7 4.1 fusion.11
  53.8 5.5 %pad_maximum_fusion = f32[256,14336]{1,0:T(8,128)} fusion(f32[256,7168]{1,0:T(8,128)S(1)} %fusion.11, f32[256,7168]{1,0:T(8,128)S(1)} %fusion.10), kind=kLoop, calls=%fused_computation.2 | loop fusion | flops 3670016 | bytes 29360128 | tf_op jit(solution)/shard_map/concatenate | solution.py:20
  59.3 0.0 reduce-scatter.3.cloned.1.call-update
  59.3 0.0 all-gather.5.cloned.1.call-start
  59.3 103.7 %reduce-scatter.3.cloned.1.call-done = f32[32,14336]{1,0:T(8,128)} async-done(((f32[256,14336]{1,0:T(8,128)}), f32[32,14336]{1,0:T(8,128)}) %reduce-scatter.3.cloned.1.call-update) | async-done | bytes 1835024 | tf_op jit(solution)/shard_map/reduce_scatter | solution.py:49
  163.1 2.5 fusion
  165.6 0.0 all-gather.5.cloned.1.call-update
  165.6 0.0 copy-start.6
  165.6 0.0 copy-start.7
  165.6 0.0 reduce-scatter.5.cloned.1.call-start
  165.7 34.4 %all-gather.5.cloned.1.call-done = bf16[256,7168]{1,0:T(8,128)(2,1)} async-done(((bf16[32,7168]{1,0:T(8,128)(2,1)}), bf16[256,7168]{1,0:T(8,128)(2,1)}) %all-gather.5.cloned.1.call-update) | async-done | bytes 3670032 | tf_op jit(solution)/shard_map/all_gather | solution.py:54
  200.1 11.2 %fusion.12 = f32[256,1024]{1,0:T(8,128)} fusion(bf16[256,7168]{1,0:T(8,128)(2,1)} %all-gather.5.cloned.1.call-done, bf16[7168,1024]{1,0:T(8,128)(2,1)} %param.18), kind=kOutput, calls=%fused_computation.37 | convolution fusion | flops 3758096384 | bytes 19398656 | tf_op jit(solution)/shard_map/dot_general | solution.py:53
  211.3 0.0 reduce-scatter.5.cloned.1.call-update
  211.4 0.0 all-gather.7.cloned.1.call-start
  211.4 0.1 fusion.4
  211.5 27.3 %reduce-scatter.5.cloned.1.call-done = f32[64,1024]{1,0:T(8,128)} async-done(((f32[256,1024]{1,0:T(8,128)}), f32[64,1024]{1,0:T(8,128)}) %reduce-scatter.5.cloned.1.call-update) | async-done | bytes 262160 | tf_op jit(solution)/shard_map/reduce_scatter | solution.py:58
  238.8 1.1 multiply_reduce_fusion
  239.9 13.2 %all-reduce.2 = (f32[64]{0:T(128)S(1)}, f32[64]{0:T(128)S(1)}) all-reduce(f32[64]{0:T(128)S(1)} %fusion.4, f32[64]{0:T(128)S(1)} %multiply_reduce_fusion), channel_id=1, replica_groups=mesh['rep'=4,'tp'=8] {'tp'}, use_global_device_ids=true, to_apply=%region_12.13 | all-reduce | flops 128 | bytes 1024 | tf_op jit(solution)/shard_map/psum | solution.py:60
  253.1 1.7 multiply_convert_fusion
  254.8 0.0 all-gather.7.cloned.1.call-update
  254.8 0.0 all-gather.11.cloned.1.call-start
  254.9 0.1 fusion.6
  255.0 10.5 %all_gather.22 = bf16[64,4096]{1,0:T(8,128)(2,1)} all-gather(bf16[64,512]{1,0:T(8,128)(2,1)S(1)} %fusion.6), channel_id=1, replica_groups=mesh['rep'=4,'tp'=8] {'tp'}, dimensions={1}, use_global_device_ids=true | all-gather | bytes 589824 | tf_op jit(solution)/shard_map/all_gather | solution.py:67
  265.5 0.0 all-gather.11.cloned.1.call-update
  265.6 0.2 all-gather.9.cloned.1.call-start
  265.8 9.6 %all-gather.7.cloned.1.call-done = bf16[64,8192]{1,0:T(8,128)(2,1)} async-done(((bf16[64,1024]{1,0:T(8,128)(2,1)}), bf16[64,8192]{1,0:T(8,128)(2,1)}) %all-gather.7.cloned.1.call-update) | async-done | bytes 1048592 | tf_op jit(solution)/shard_map/all_gather | solution.py:66
  275.4 0.0 all-gather.9.cloned.1.call-update
  275.5 0.7 gather_fusion
  276.3 0.1 broadcast_select_fusion
  276.4 20.6 %convert_reduce_fusion = f32[256,2048]{1,0:T(8,128)} fusion(s32[2048]{0:T(1024)S(1)} %iota_add_fusion, s32[256,24]{1,0:T(8,128)S(1)} %broadcast_select_fusion), kind=kLoop, calls=%fused_computation.1 | loop fusion | flops 37224448 | bytes 2129920 | tf_op jit(solution)/shard_map/reduce_sum | solution.py:91
  297.0 25.5 %all-gather.11.cloned.1.call-done = bf16[256,4096]{1,0:T(8,128)(2,1)} async-done(((bf16[64,4096]{1,0:T(8,128)(2,1)}), bf16[256,4096]{1,0:T(8,128)(2,1)}) %all-gather.11.cloned.1.call-update) | async-done | bytes 2097168 | tf_op jit(solution)/shard_map/all_gather | solution.py:71
  322.5 8.8 %fusion.8 = (f32[256]{0:T(256)S(1)}, f32[256,2048]{1,0:T(8,128)S(1)}) fusion(bf16[256,4096]{1,0:T(8,128)(2,1)} %all-gather.11.cloned.1.call-done, bf16[4096,2048]{1,0:T(8,128)(2,1)} %param.23, f32[256]{0:T(256)S(1)} %copy-done.9), kind=kOutput, calls=%fused_computation.33 | convolution fusion | flops 4296015872 | bytes 20973568 | tf_op jit(solution)/shard_map/dot_general | solution.py:76
  331.3 72.2 %all-gather.9.cloned.1.call-done = bf16[256,8192]{1,0:T(8,128)(2,1)} async-done(((bf16[64,8192]{1,0:T(8,128)(2,1)}), bf16[256,8192]{1,0:T(8,128)(2,1)}) %all-gather.9.cloned.1.call-update) | async-done | bytes 4194320 | tf_op jit(solution)/shard_map/all_gather | solution.py:70
  403.5 17.2 %fusion.9 = (f32[256]{0:T(256)S(1)}, f32[256,2048]{1,0:T(8,128)}) fusion(bf16[256,8192]{1,0:T(8,128)(2,1)} %all-gather.9.cloned.1.call-done, bf16[8192,2048]{1,0:T(8,128)(2,1)} %param.20, f32[256]{0:T(256)S(1)} %copy-done.9), kind=kOutput, calls=%fused_computation.34 | convolution fusion | flops 8590983168 | bytes 39847936 | tf_op jit(solution)/shard_map/dot_general | solution.py:73
  420.7 38.6 %all-reduce = (f32[256]{0:T(256)S(1)}, f32[256]{0:T(256)S(1)}) all-reduce(f32[256]{0:T(256)S(1)} %get-tuple-element.12, f32[256]{0:T(256)S(1)} %get-tuple-element.14), channel_id=1, replica_groups=mesh['rep'=4,'tp'=8] {'rep','tp'}, use_global_device_ids=true, to_apply=%region_14.15 | all-reduce | flops 512 | bytes 4096 | tf_op jit(solution)/shard_map/pmax | solution.py:79
  459.4 2.3 exponential_reduce_fusion
  461.7 12.7 %all-reduce.1 = (f32[256]{0:T(256)S(1)}, f32[256]{0:T(256)S(1)}) all-reduce(f32[256]{0:T(256)S(1)} %get-tuple-element.16, f32[256]{0:T(256)S(1)} %get-tuple-element.17), channel_id=1, replica_groups=mesh['rep'=4,'tp'=8] {'tp'}, use_global_device_ids=true, to_apply=%region_16.17 | all-reduce | flops 512 | bytes 4096 | tf_op jit(solution)/shard_map/psum | solution.py:84
  474.4 10.6 %all-reduce.3 = (f32[256]{0:T(256)S(1)}, f32[256]{0:T(256)S(1)}) all-reduce(f32[256]{0:T(256)S(1)} %get-tuple-element.4, f32[256]{0:T(256)S(1)} %get-tuple-element.5), channel_id=1, replica_groups=mesh['rep'=4,'tp'=8] {'rep'}, use_global_device_ids=true, to_apply=%region_17.18 | all-reduce | flops 512 | bytes 4096 | tf_op jit(solution)/shard_map/psum | solution.py:84
  485.0 4.4 fusion.7
  489.3 37.4 %pmax.23 = f32[256]{0:T(256)} all-reduce(f32[256]{0:T(256)S(1)} %get-tuple-element.10), channel_id=1, replica_groups=mesh['rep'=4,'tp'=8] {'rep','tp'}, use_global_device_ids=true, to_apply=%region_20.21 | all-reduce | flops 256 | bytes 2048 | tf_op jit(solution)/shard_map/pmax | solution.py:96
  (26 shorter events, 0.1 us)
Async XLA Ops:
  7.2 268.3 %copy-start = (s32[8,24]{1,0:T(8,128)S(1)}, s32[8,24]{1,0:T(8,128)}, u32[]{:S(2)}) copy-start(s32[8,24]{1,0:T(8,128)} %param.26) | copy-start | bytes 2308
  7.2 155.9 %reduce-scatter.3.cloned.1.call-start = ((), (), s32[]{:S(2)}) async-start(), calls=%async_computation.2 | async-start | bytes 16515072 | tf_op jit(solution)/shard_map/reduce_scatter | solution.py:49
  40.4 9.3 %copy-start.2 = (bf16[1024,7168]{1,0:T(8,128)(2,1)S(1)}, bf16[1024,7168]{1,0:T(8,128)(2,1)}, u32[]{:S(2)}) copy-start(bf16[1024,7168]{1,0:T(8,128)(2,1)} %param.17) | copy-start | bytes 44040196
  59.3 140.8 %all-gather.5.cloned.1.call-start = ((), (), s32[]{:S(2)}) async-start(), calls=%async_computation.3 | async-start | bytes 4128768 | tf_op jit(solution)/shard_map/all_gather | solution.py:54
  165.6 45.8 %copy-start.4 = (bf16[64,512]{1,0:T(8,128)(2,1)S(1)}, bf16[64,512]{1,0:T(8,128)(2,1)}, u32[]{:S(2)}) copy-start(bf16[64,512]{1,0:T(8,128)(2,1)} %param.21) | copy-start | bytes 196612
  165.6 73.2 %copy-start.3 = (bf16[64,1024]{1,0:T(8,128)(2,1)S(1)}, bf16[64,1024]{1,0:T(8,128)(2,1)}, u32[]{:S(2)}) copy-start(bf16[64,1024]{1,0:T(8,128)(2,1)} %param.14) | copy-start | bytes 393220
  165.6 87.5 %copy-start.6 = (f32[1024]{0:T(1024)S(1)}, f32[1024]{0:T(1024)}, u32[]{:S(2)}) copy-start(f32[1024]{0:T(1024)} %param.19) | copy-start | bytes 12292
  165.6 89.3 %copy-start.7 = (f32[512]{0:T(512)S(1)}, f32[512]{0:T(512)}, u32[]{:S(2)}) copy-start(f32[512]{0:T(512)} %param.22) | copy-start | bytes 6148
  165.6 73.2 %reduce-scatter.5.cloned.1.call-start = ((), (), s32[]{:S(2)}) async-start(), calls=%async_computation.4 | async-start | bytes 1310720 | tf_op jit(solution)/shard_map/reduce_scatter | solution.py:58
  211.3 64.1 %copy-start.8 = (s32[256]{0:T(256)S(1)}, s32[256]{0:T(256)}, u32[]{:S(2)}) copy-start(s32[256]{0:T(256)} %param.25) | copy-start | bytes 3076
  211.3 64.9 %copy-start.5 = (s32[2048]{0:T(1024)S(1)}, s32[2048]{0:T(1024)}, u32[]{:S(2)}) copy-start(s32[2048]{0:T(1024)} %param.27) | copy-start | bytes 24580
  211.4 111.2 %copy-start.9 = (f32[256]{0:T(256)S(1)}, f32[256]{0:T(256)}, u32[]{:S(2)}) copy-start(f32[256]{0:T(256)} %param.24) | copy-start | bytes 3076
  211.4 64.0 %all-gather.7.cloned.1.call-start = ((), (), s32[]{:S(2)}) async-start(), calls=%async_computation.5 | async-start | bytes 1179648 | tf_op jit(solution)/shard_map/all_gather | solution.py:66
  254.8 67.7 %all-gather.11.cloned.1.call-start = ((), (), s32[]{:S(2)}) async-start(), calls=%async_computation.7 | async-start | bytes 2621440 | tf_op jit(solution)/shard_map/all_gather | solution.py:71
  265.6 138.0 %all-gather.9.cloned.1.call-start = ((), (), s32[]{:S(2)}) async-start(), calls=%async_computation.6 | async-start | bytes 5242880 | tf_op jit(solution)/shard_map/all_gather | solution.py:70
  485.0 41.8 %copy-start.1 = (s32[8,24]{1,0:T(8,128)S(1)}, s32[8,24]{1,0:T(8,128)}, u32[]{:S(2)}) copy-start(s32[8,24]{1,0:T(8,128)} %param.26) | copy-start | bytes 2308
Sparse Core Ops, SparseCore 0:
  59.4 103.6 reduce-scatter.2
  165.7 34.3 all-gather.4
  211.5 27.2 reduce-scatter.4
  255.0 20.3 all-gather.6
  276.8 45.6 all-gather.10
  323.9 79.5 all-gather.8
